TPU v7x, 32 devices: a whole 2x2x4 slice. The times are simulated.
32 devices in a mesh: groups: 2 (over y), center: 8 (over z, x), row: 2 (over core).
Axes of the slice: x: 2, y: 2, z: 4, core: 2. Of those that a mesh axis runs over, the one named last changes fastest.
Arguments:
- dataset: float32 [512, 1024], P(('groups', 'center', 'row')), parts along dimension 0, may hold values from -0.1875 to 0.1875
- centers: float32 [2048, 1024], P(('groups', 'center')), parts along dimension 0, may hold values from -0.1875 to 0.1875
- weights: float32 [2048, 512], P(('groups', 'center'), 'row'), parts along dimension 0, may hold values from -0.1875 to 0.1875
- batch_index: int32 [2, 128], P(None, ('groups', 'center', 'row')), parts along dimension 1, may hold values from 0 to 15
- targets: float32 [2, 128, 512], P(None, ('groups', 'center', 'row')), parts along dimension 1, may hold values from -6 to 6
- gamma: float32 [2], P('groups'), parts along dimension 0, may hold values from 0.3 to 1.5
Outputs:
- new_weights: float32 [2048, 512], P(('groups', 'center'), 'row'), parts along dimension 0
- residual: float32 [128, 512], P(('groups', 'center', 'row')), parts along dimension 0
There are 2 independent parts, one for each index of `groups`. A program takes and returns all parts, laid end to end along the dimension named above; each array names one. Nothing has to cross between parts.
Inputs may be any that keep to these rules, and one draw needn't show every extreme that they name: `batch_index`: each entry picks a row within the block of 16 dataset rows that has the same block number as the entry's block of 4 batch rows.
All inputs are finite; a program needn't handle non-finite values.
Results may differ from a plain program's by a relative error of at most 0.0001.
Values sent between devices are 32-bit elements; how exact they have to be, the bound alone decides.
No kernel may reach another device: no remote copies, remote signals or barrier semaphores. Data moves between devices by JAX's collectives and lax.ppermute only.
A program may use at most 64 MiB of HBM per device.

v0:
```python
import jax
import jax.numpy as jnp
from jax import lax
from jax.sharding import PartitionSpec as P


def per_device(dataset, centers, weights, batch_index, targets, gamma):
    center_sq = jnp.sum(centers * centers, axis=1)
    rows_here = batch_index.shape[1]
    current = weights
    residual = None
    for step in range(2):
        local_rows = dataset[batch_index[step]]
        rows, wanted = (
            lax.all_gather(local_rows, "center", axis=0, tiled=True),
            lax.all_gather(targets[step], "center", axis=0, tiled=True),
        )
        full_weights = lax.all_gather(current, "row", axis=1, tiled=True)
        row_sq = jnp.sum(rows * rows, axis=1)
        cross = jnp.dot(
            rows, centers.T, precision=lax.Precision.HIGHEST, preferred_element_type=jnp.float32
        )
        kernel = jnp.exp(-gamma[0] * (row_sq[:, None] + center_sq[None, :] - 2.0 * cross))
        partial_pred = jnp.dot(
            kernel,
            full_weights,
            precision=lax.Precision.HIGHEST,
            preferred_element_type=jnp.float32,
        )
        summed = lax.psum(partial_pred, "center")
        gathered_res = summed - wanted
        residual = lax.dynamic_slice_in_dim(
            gathered_res, lax.axis_index("center") * rows_here, rows_here, 0
        )
        grad = jnp.dot(
            kernel.T,
            gathered_res,
            precision=lax.Precision.HIGHEST,
            preferred_element_type=jnp.float32,
        )
        own_grad = lax.psum_scatter(grad, "row", scatter_dimension=1, tiled=True)
        batch_total = rows.shape[0] * lax.axis_size("row")
        current = current - 0.5 / batch_total * own_grad
    return (current, residual)


def solution(mesh):
    return jax.shard_map(
        per_device,
        mesh=mesh,
        in_specs=(
            P(("groups", "center", "row"), None),
            P(("groups", "center"), None),
            P(("groups", "center"), "row"),
            P(None, ("groups", "center", "row")),
            P(None, ("groups", "center", "row"), None),
            P("groups"),
        ),
        out_specs=(P(("groups", "center"), "row"), P(("groups", "center", "row"), None)),
        check_vma=False,
    )
```

profile of v0, /device:TPU:0, one launch (start us, length us, event | category | flops | bytes accessed | tf_op | source)
XLA Modules:
  0.0 241.9 jit_solution(545532573906874737)
XLA Ops:
  7.2 0.0 copy-start
  7.2 0.0 all-reduce.3.cloned.1.call-start
  7.9 0.0 copy-start.4
  7.9 1.2 multiply_reduce_fusion
  9.0 0.0 copy-done.4
  9.1 0.0 copy-done
  9.1 0.0 copy-start.1
  9.1 0.6 gather_fusion
  9.7 32.3 %all-gather.4 = f32[8,4,1024]{2,1,0:T(4,128)S(1)} all-gather(f32[1,4,1024]{2,1,0:T(4,128)S(1)} %bitcast.27), channel_id=2, replica_groups=mesh['groups'=2,'center'=8,'row'=2] {'center'}, dimensions={0}, use_global_device_ids=true | all-gather | bytes 147456 | tf_op jit(solution)/shard_map/all_gather | solution.py:15
  42.1 0.0 copy-start.2
  42.1 0.1 multiply_reduce_fusion.2
  42.2 0.8 copy-done.2
  43.0 2.0 all_gather.19
  44.9 0.0 copy-done.1
  44.9 0.6 fusion.5
  45.6 0.9 fusion.11
  46.5 0.0 copy-start.3
  46.5 0.0 all-reduce.3.cloned.1.call-update
  46.5 0.0 reduce-scatter.3.cloned.1.call-start
  46.5 0.6 copy-done.3
  47.2 30.5 %all-gather.1 = f32[1,32,512]{2,0,1:T(1,128)S(1)} all-gather(f32[1,4,512]{2,0,1:T(1,128)S(1)} %copy.12), channel_id=3, replica_groups=mesh['groups'=2,'center'=8,'row'=2] {'center'}, dimensions={1}, use_global_device_ids=true | all-gather | bytes 73728 | tf_op jit(solution)/shard_map/all_gather | solution.py:16
  77.7 39.1 %all-reduce.3.cloned.1.call-done = f32[32,512]{1,0:T(8,128)} async-done(((f32[32,512]{1,0:T(8,128)}), f32[32,512]{1,0:T(8,128)}) %all-reduce.3.cloned.1.call-update) | async-done | bytes 65552 | tf_op jit(solution)/shard_map/psum | solution.py:30
  116.8 2.0 fusion.6
  118.8 0.0 reduce-scatter.3.cloned.1.call-update
  118.8 0.0 all-reduce.5.cloned.1.call-start
  118.8 0.6 gather_fusion.1
  119.4 30.5 %all-gather.5 = f32[8,4,1024]{2,1,0:T(4,128)S(1)} all-gather(f32[1,4,1024]{2,1,0:T(4,128)S(1)} %bitcast.28), channel_id=4, replica_groups=mesh['groups'=2,'center'=8,'row'=2] {'center'}, dimensions={0}, use_global_device_ids=true | all-gather | bytes 147456 | tf_op jit(solution)/shard_map/all_gather | solution.py:15
  150.0 0.1 multiply_reduce_fusion.1
  150.1 0.6 fusion.2
  150.8 0.0 reduce-scatter.3.cloned.1.call-done
  150.8 0.9 multiply_subtract_fusion.1
  151.7 2.0 all_gather.22
  153.7 0.9 fusion.12
  154.6 0.0 all-reduce.5.cloned.1.call-update
  154.6 0.0 reduce-scatter.5.cloned.1.call-start
  154.7 30.5 %all-gather.3 = f32[1,32,512]{2,0,1:T(1,128)S(1)} all-gather(f32[1,4,512]{2,0,1:T(1,128)S(1)} %copy.13), channel_id=5, replica_groups=mesh['groups'=2,'center'=8,'row'=2] {'center'}, dimensions={1}, use_global_device_ids=true | all-gather | bytes 73728 | tf_op jit(solution)/shard_map/all_gather | solution.py:16
  185.2 38.8 %all-reduce.5.cloned.1.call-done = f32[32,512]{1,0:T(8,128)} async-done(((f32[32,512]{1,0:T(8,128)}), f32[32,512]{1,0:T(8,128)}) %all-reduce.5.cloned.1.call-update) | async-done | bytes 65552 | tf_op jit(solution)/shard_map/psum | solution.py:30
  224.0 0.8 bitcast_subtract_fusion
  224.8 1.1 fusion.13
  226.0 0.0 reduce-scatter.5.cloned.1.call-update
  226.0 0.6 constant_dynamic-slice_fusion
  226.6 7.2 %reduce-scatter.5.cloned.1.call-done = f32[128,256]{1,0:T(8,128)} async-done(((f32[128,512]{1,0:T(8,128)}), f32[128,256]{1,0:T(8,128)}) %reduce-scatter.5.cloned.1.call-update) | async-done | bytes 131088 | tf_op jit(solution)/shard_map/reduce_scatter | solution.py:41
  233.8 1.6 multiply_subtract_fusion
  (7 shorter events, 0.1 us)
Async XLA Ops:
  7.2 1.9 copy-start
  7.2 109.6 %all-reduce.3.cloned.1.call-start = ((), (), s32[]{:S(2)}) async-start(), calls=%async_computation.2 | async-start | bytes 131072 | tf_op jit(solution)/shard_map/psum | solution.py:30
  7.9 1.2 copy-start.4
  9.1 35.9 %copy-start.1 = (f32[128,1024]{1,0:T(8,128)S(1)}, f32[128,1024]{1,0:T(8,128)}, u32[]{:S(2)}) copy-start(f32[128,1024]{1,0:T(8,128)} %param.7) | copy-start | bytes 1572868
  42.1 0.9 copy-start.2
  46.5 0.7 copy-start.3
  46.5 104.3 %reduce-scatter.3.cloned.1.call-start = ((), (), s32[]{:S(2)}) async-start(), calls=%async_computation.3 | async-start | bytes 393216 | tf_op jit(solution)/shard_map/reduce_scatter | solution.py:41
  118.8 105.2 %all-reduce.5.cloned.1.call-start = ((), (), s32[]{:S(2)}) async-start(), calls=%async_computation.4 | async-start | bytes 131072 | tf_op jit(solution)/shard_map/psum | solution.py:30
  154.6 79.2 %reduce-scatter.5.cloned.1.call-start = ((), (), s32[]{:S(2)}) async-start(), calls=%async_computation.5 | async-start | bytes 393216 | tf_op jit(solution)/shard_map/reduce_scatter | solution.py:41
Sparse Core Ops, SparseCore 0:
  46.6 70.1 all-reduce.2
  119.0 7.6 reduce-scatter.2
  154.7 69.2 all-reduce.4
  226.1 7.6 reduce-scatter.4
where the time goes:
time: 242 us
  blocking collectives  128 us (53%)
  waiting for transfers between devices  85.2 us (35%)
  between operations  14.5 us (6%)
  matrix products  6.1 us (3%)
  other arithmetic  4.76 us (2%)
  local copies, waits for them, and re-layouts  3.3 us (1%)
    psum x2, waiting for transfers between devices, per_device(): summed = lax.psum(partial_pred, 'center')  77.8 us
    all_gather x2, blocking collectives, per_device(): lax.all_gather(local_rows, 'center', axis=0, tiled=True)  62.9 us
    all_gather x2, blocking collectives, per_device(): lax.all_gather(targets[step], 'center', axis=0, tiled=True)  61.1 us
    reduce_scatter x2, waiting for transfers between devices, per_device(): own_grad = lax.psum_scatter(grad, 'row', scatter_dimension=1, tiled=True)  7.25 us
  transfers between devices with their start and end apart: 4, of which 3 were waited for; matrix products, arithmetic and copies ran while one was open for 1% of the time, Pallas kernels for 0%

commit v1 on v0

--- a/solution.py
+++ b/solution.py
@@ -2,6 +2,12 @@
 import jax.numpy as jnp
 from jax import lax
 from jax.sharding import PartitionSpec as P
+
+
+def add_all(x, axis):
+    parts = lax.all_gather(x, axis, axis=0, tiled=False)
+    acc = parts.sum(axis=0)
+    return acc
 
 
 def per_device(dataset, centers, weights, batch_index, targets, gamma):
@@ -27,7 +33,7 @@
             precision=lax.Precision.HIGHEST,
             preferred_element_type=jnp.float32,
         )
-        summed = lax.psum(partial_pred, "center")
+        summed = add_all(partial_pred, "center")
         gathered_res = summed - wanted
         residual = lax.dynamic_slice_in_dim(
             gathered_res, lax.axis_index("center") * rows_here, rows_here, 0

time: 242 us -> 224 us (0.926)
  waiting for transfers between devices: 85.2 us -> 8.23 us
  blocking collectives: 128 us -> 191 us
    psum x2 -> x0, waiting for transfers between devices: 77.8 us -> none  [per_device(): summed = lax.psum(partial_pred, 'center')]
    all_gather x0 -> x2, blocking collectives: none -> 62.8 us  [add_all(): parts = lax.all_gather(x, axis, axis=0, tiled=False)]
  transfers between devices with their start and end apart: 4 -> 2, of which waited for: 3 -> 1; matrix products, arithmetic and copies ran while one was open for 1% -> 1% of each run, Pallas kernels for 0% -> 0%
where the time goes in v1:
time: 224 us
  blocking collectives  191 us (85%)
  between operations  14.8 us (7%)
  waiting for transfers between devices  8.23 us (4%)
  matrix products  3.97 us (2%)
  other arithmetic  3.7 us (2%)
  local copies, waits for them, and re-layouts  2.66 us (1%)
    all_gather x2, blocking collectives, per_device(): lax.all_gather(local_rows, 'center', axis=0, tiled=True)  62.9 us
    all_gather x2, blocking collectives, add_all(): parts = lax.all_gather(x, axis, axis=0, tiled=False)  62.8 us
    all_gather x2, blocking collectives, per_device(): lax.all_gather(targets[step], 'center', axis=0, tiled=True)  61.1 us
    reduce_scatter x2, waiting for transfers between devices, per_device(): own_grad = lax.psum_scatter(grad, 'row', scatter_dimension=1, tiled=True)  8.2 us
  transfers between devices with their start and end apart: 2, of which 1 were waited for; matrix products, arithmetic and copies ran while one was open for 1% of the time, Pallas kernels for 0%

profile of v1, /device:TPU:0, one launch (start us, length us, event | category | flops | bytes accessed | tf_op | source)
XLA Modules:
  0.0 224.2 jit_solution(14686264214478952327)
XLA Ops:
  7.2 0.0 copy-start
  7.2 0.0 copy-start.1
  7.2 0.0 reduce-scatter.3.cloned.1.call-start
  7.2 0.8 fusion.9
  8.0 0.0 copy-done
  8.0 0.6 gather_fusion
  8.6 32.3 %all-gather.6 = f32[8,4,1024]{2,1,0:T(4,128)S(1)} all-gather(f32[1,4,1024]{2,1,0:T(4,128)S(1)} %bitcast.31), channel_id=2, replica_groups=mesh['groups'=2,'center'=8,'row'=2] {'center'}, dimensions={0}, use_global_device_ids=true | all-gather | bytes 147456 | tf_op jit(solution)/shard_map/all_gather | solution.py:21
  41.0 0.1 multiply_reduce_fusion.2
  41.7 0.0 copy-done.1
  41.8 0.0 copy-start.2
  41.8 0.1 multiply_reduce_fusion
  41.9 0.8 copy-done.2
  42.7 2.0 all_gather.31
  44.6 0.6 fusion.5
  45.3 0.2 fusion.11
  45.5 0.0 copy-start.3
  45.5 31.4 %all-gather.1 = f32[256,512]{1,0:T(8,128)S(1)} all-gather(f32[32,512]{1,0:T(8,128)S(1)} %fusion.11), channel_id=3, replica_groups=mesh['groups'=2,'center'=8,'row'=2] {'center'}, dimensions={0}, use_global_device_ids=true | all-gather | bytes 589824 | tf_op jit(solution)/shard_map/all_gather | solution.py:8
  77.0 0.0 copy-done.3
  77.0 30.5 %all-gather.2 = f32[1,32,512]{2,0,1:T(1,128)S(1)} all-gather(f32[1,4,512]{2,0,1:T(1,128)S(1)} %copy.12), channel_id=4, replica_groups=mesh['groups'=2,'center'=8,'row'=2] {'center'}, dimensions={1}, use_global_device_ids=true | all-gather | bytes 73728 | tf_op jit(solution)/shard_map/all_gather | solution.py:22
  107.6 1.1 fusion.6
  108.7 0.0 reduce-scatter.3.cloned.1.call-update
  108.7 0.0 reduce-scatter.5.cloned.1.call-start
  108.7 0.6 gather_fusion.1
  109.3 30.5 %all-gather.7 = f32[8,4,1024]{2,1,0:T(4,128)S(1)} all-gather(f32[1,4,1024]{2,1,0:T(4,128)S(1)} %bitcast.32), channel_id=5, replica_groups=mesh['groups'=2,'center'=8,'row'=2] {'center'}, dimensions={0}, use_global_device_ids=true | all-gather | bytes 147456 | tf_op jit(solution)/shard_map/all_gather | solution.py:21
  139.9 30.5 %all-gather.5 = f32[1,32,512]{2,0,1:T(1,128)S(1)} all-gather(f32[1,4,512]{2,0,1:T(1,128)S(1)} %copy.13), channel_id=7, replica_groups=mesh['groups'=2,'center'=8,'row'=2] {'center'}, dimensions={1}, use_global_device_ids=true | all-gather | bytes 73728 | tf_op jit(solution)/shard_map/all_gather | solution.py:22
  170.4 0.1 multiply_reduce_fusion.1
  170.6 0.6 fusion.2
  171.2 0.0 reduce-scatter.3.cloned.1.call-done
  171.2 0.9 multiply_subtract_fusion.1
  172.2 2.0 all_gather.36
  174.1 0.2 fusion.12
  174.4 31.4 %all-gather.4 = f32[256,512]{1,0:T(8,128)S(1)} all-gather(f32[32,512]{1,0:T(8,128)S(1)} %fusion.12), channel_id=6, replica_groups=mesh['groups'=2,'center'=8,'row'=2] {'center'}, dimensions={0}, use_global_device_ids=true | all-gather | bytes 589824 | tf_op jit(solution)/shard_map/all_gather | solution.py:8
  205.8 1.1 fusion.13
  206.9 0.0 reduce-scatter.5.cloned.1.call-update
  207.0 0.6 constant_dynamic-slice_fusion
  207.6 8.2 %reduce-scatter.5.cloned.1.call-done = f32[128,256]{1,0:T(8,128)} async-done(((f32[128,512]{1,0:T(8,128)}), f32[128,256]{1,0:T(8,128)}) %reduce-scatter.5.cloned.1.call-update) | async-done | bytes 131088 | tf_op jit(solution)/shard_map/reduce_scatter | solution.py:47
  215.8 1.6 multiply_subtract_fusion
  (9 shorter events, 0.2 us)
Async XLA Ops:
  7.2 0.8 copy-start
  7.2 34.6 %copy-start.1 = (f32[128,1024]{1,0:T(8,128)S(1)}, f32[128,1024]{1,0:T(8,128)}, u32[]{:S(2)}) copy-start(f32[128,1024]{1,0:T(8,128)} %param.7) | copy-start | bytes 1572868
  7.2 164.0 %reduce-scatter.3.cloned.1.call-start = ((), (), s32[]{:S(2)}) async-start(), calls=%async_computation.2 | async-start | bytes 393216 | tf_op jit(solution)/shard_map/reduce_scatter | solution.py:47
  41.8 0.9 copy-start.2
  45.5 31.4 %copy-start.3 = (f32[2,4,512]{2,1,0:T(4,128)S(1)}, f32[2,4,512]{2,1,0:T(4,128)}, u32[]{:S(2)}) copy-start(f32[2,4,512]{2,1,0:T(4,128)} %param.10) | copy-start | bytes 49156
  108.7 107.1 %reduce-scatter.5.cloned.1.call-start = ((), (), s32[]{:S(2)}) async-start(), calls=%async_computation.3 | async-start | bytes 393216 | tf_op jit(solution)/shard_map/reduce_scatter | solution.py:47
Sparse Core Ops, SparseCore 0:
  108.8 8.5 reduce-scatter.2
  207.1 8.6 reduce-scatter.4
